TPU v7x, 32 devices: a whole 2x2x4 slice. The times are simulated.
32 devices in a mesh: groups: 2 (over x), expert: 16 (over z, y, core).
Axes of the slice: x: 2, y: 2, z: 4, core: 2. Of those that a mesh axis runs over, the one named last changes fastest.
Arguments:
- tokens: bfloat16 [1024, 2048], P(('groups', 'expert')), parts along dimension 0, may hold values from -6 to 6
- expert_ids: int32 [1024, 2], P(('groups', 'expert')), parts along dimension 0, may hold values from 0 to 7, all different within a row; in each aligned block of 32 rows (0 to 31, 32 to 63, ...) at most 16 rows name the same one
- member_ids: int32 [1024], P(('groups', 'expert')), parts along dimension 0, may hold values from 0 to 7
- combine_weights: float32 [1024, 2], P(('groups', 'expert')), parts along dimension 0, may hold values from 0.25 to 1
- gate_weight: bfloat16 [2048, 57344], P(None, 'expert'), may hold values from -0.125 to 0.125
- up_weight: bfloat16 [2048, 57344], P(None, 'expert'), may hold values from -0.125 to 0.125
- down_weight: bfloat16 [57344, 2048], P('expert'), may hold values from -0.0625 to 0.0625
- input_factors: float32 [8, 8, 4096], replicated, may hold values from 0.5 to 2
- hidden_factors: float32 [8, 2, 57344], P(None, None, 'expert'), may hold values from 0.5 to 2
- output_factors: float32 [8, 8, 2048], replicated, may hold values from 0.5 to 2
Outputs:
- mixed: bfloat16 [1024, 2048], P(('groups', 'expert')), parts along dimension 0
There are 2 independent parts, one for each index of `groups`. A program takes and returns all parts, laid end to end along the dimension named above; an argument that names none is the same for every part. Nothing has to cross between parts.
Inputs may be any that keep to these rules, and one draw needn't show every extreme that they name: `expert_ids`: the two experts of a token differ. Among the 32 tokens of one device no expert is named more than 16 times.
All inputs are finite; a program needn't handle non-finite values.
Results may differ from a plain program's by a relative error of at most 0.012.
Values may be sent and summed in bfloat16 or wider, within the bound.
A program may use at most 128 MiB of HBM per device.

v0:
```python
import jax
import jax.numpy as jnp
from jax import lax
from jax.sharding import PartitionSpec as P

EXPERTS = 8
MEMBERS = 8
CAP = 16


def swapped(block, axis, apart):
    count = lax.axis_size(axis)
    route = []
    for low in range(count):
        high = low | 1 << apart
        if high != low and high < count:
            route += [(low, high), (high, low)]
    return lax.ppermute(block, axis, route)


def lookup(select, table):
    return jnp.dot(
        select, table, precision=lax.Precision.HIGHEST, preferred_element_type=jnp.float32
    )


def expert_rows(
    row_data,
    plus_member,
    own_expert,
    gate_weight,
    up_weight,
    down_weight,
    input_factors,
    hidden_factors,
):
    members = input_factors.shape[1]
    width = row_data.shape[1]
    units = gate_weight.shape[1]
    select = (
        plus_member.astype(jnp.float32)[:, None] - 1.0
        == jnp.arange(members, dtype=jnp.float32)[None, :]
    ).astype(jnp.float32)
    in_table = lax.dynamic_index_in_dim(input_factors, own_expert, 0, keepdims=False)
    in_scale = lookup(select, in_table)
    gate_in = (row_data * in_scale[:, :width]).astype(jnp.bfloat16)
    up_in = (row_data * in_scale[:, width:]).astype(jnp.bfloat16)
    gate = jnp.dot(gate_in, gate_weight, preferred_element_type=jnp.float32)
    up = jnp.dot(up_in, up_weight, preferred_element_type=jnp.float32)
    hid_scale = lookup(select, hidden_factors.reshape(members, 2 * units))
    hidden = (jax.nn.silu(gate * hid_scale[:, :units]) * (up * hid_scale[:, units:])).astype(
        jnp.bfloat16
    )
    return jnp.dot(hidden, down_weight, preferred_element_type=jnp.float32).astype(jnp.bfloat16)


def run_rows(
    row_data,
    plus_member,
    own_expert,
    gate_weight,
    up_weight,
    down_weight,
    input_factors,
    hidden_factors,
):
    return expert_rows(
        row_data,
        plus_member,
        own_expert,
        gate_weight,
        up_weight,
        down_weight,
        input_factors,
        hidden_factors,
    )


def send_back(partial_value, position, split):
    devices = partial_value.shape[0]
    slots = partial_value.shape[1]
    width = partial_value.shape[2]
    held = partial_value.astype(jnp.float32)
    levels = split.bit_length() - 1
    for level in range(levels):
        bit = levels - 1 - level
        half = held.shape[1] // 2
        lower = held[:, :half]
        higher = held[:, half:]
        upper = position // 2**bit % 2 == 1
        keep = jnp.where(upper, higher, lower)
        give = jnp.where(upper, lower, higher)
        held = keep + swapped(give.astype(jnp.bfloat16), "expert", bit).astype(give.dtype)
    arrived = lax.all_to_all(
        held.astype(jnp.bfloat16), "expert", split_axis=0, concat_axis=0, tiled=True
    ).astype(held.dtype)
    return arrived.reshape(devices // split * slots, width)


def per_device(
    tokens,
    expert_ids,
    member_ids,
    combine_weights,
    gate_weight,
    up_weight,
    down_weight,
    input_factors,
    hidden_factors,
    output_factors,
):
    devices = lax.axis_size("expert")
    split = devices // EXPERTS
    position = lax.axis_index("expert")
    own_expert = position // split
    tok_count = tokens.shape[0]
    width = tokens.shape[1]
    flat_expert = expert_ids.reshape(-1)
    expert_hits = (flat_expert[:, None] == jnp.arange(EXPERTS, dtype=jnp.int32)[None, :]).astype(
        jnp.int32
    )
    slot_index = jnp.sum((jnp.cumsum(expert_hits, 0) - 1) * expert_hits, 1)
    target = flat_expert * CAP + slot_index
    placing = (jnp.arange(EXPERTS * CAP, dtype=jnp.int32)[:, None] == target[None, :]).astype(
        jnp.float32
    )
    by_token = placing.reshape(EXPERTS * CAP, tok_count, 2).sum(2)
    send_rows = jnp.dot(
        by_token.astype(jnp.bfloat16), tokens, preferred_element_type=jnp.float32
    ).astype(jnp.bfloat16)
    send_member = jnp.dot(
        by_token, (member_ids + 1).astype(jnp.float32), precision=lax.Precision.HIGHEST
    ).astype(jnp.bfloat16)
    rows_out = jnp.repeat(send_rows.reshape(EXPERTS, CAP, width), split, axis=0)
    member_out = jnp.repeat(send_member.reshape(EXPERTS, CAP, 1), split, axis=0)
    row_piece, member_piece = (
        lax.all_to_all(rows_out, "expert", split_axis=0, concat_axis=0, tiled=True),
        lax.all_to_all(member_out, "expert", split_axis=0, concat_axis=0, tiled=True),
    )
    partial_value = run_rows(
        row_piece.reshape(devices * CAP, width),
        member_piece.reshape(devices * CAP),
        own_expert,
        gate_weight,
        up_weight,
        down_weight,
        input_factors,
        hidden_factors,
    )
    summed = send_back(partial_value.reshape(devices, CAP, width), position, split)
    picked = jnp.dot(
        placing.T, summed, precision=lax.Precision.HIGHEST, preferred_element_type=jnp.float32
    )
    pair_member = jnp.repeat(member_ids, 2)
    factor_hits = (
        (flat_expert * MEMBERS + pair_member)[:, None]
        == jnp.arange(EXPERTS * MEMBERS, dtype=jnp.int32)[None, :]
    ).astype(jnp.float32)
    out_scale = lookup(factor_hits, output_factors.reshape(EXPERTS * MEMBERS, width))
    weighted = picked * out_scale * combine_weights.reshape(-1)[:, None]
    return weighted.reshape(tok_count, 2, width).sum(1).astype(jnp.bfloat16)


def solution(mesh):
    in_specs = (
        P(("groups", "expert"), None),
        P(("groups", "expert"), None),
        P(("groups", "expert")),
        P(("groups", "expert"), None),
        P(None, "expert"),
        P(None, "expert"),
        P("expert", None),
        P(),
        P(None, None, "expert"),
        P(),
    )
    out_specs = P(("groups", "expert"), None)
    return jax.shard_map(
        per_device, mesh=mesh, in_specs=in_specs, out_specs=out_specs, check_vma=False
    )
```

profile of v0, /device:TPU:0, one launch (start us, length us, event | category | flops | bytes accessed | tf_op | source)
XLA Modules:
  0.0 101.5 jit_solution(2548334407414446849)
XLA Ops:
  0.0 0.9 copy.34
  1.5 0.7 multiply_add_fusion
  2.3 0.8 fusion.5
  3.2 0.6 copy.36
  3.8 7.4 %all-to-all-start.1 = ((bf16[16,16,1]{1,2,0:T(2,128)(2,1)}), bf16[16,16,1]{1,2,0:T(2,128)(2,1)S(1)}, u32[]{:S(2)}, u32[]{:S(2)}) async-start(bf16[16,16,1]{1,2,0:T(2,128)(2,1)} %copy.36), calls=%async_computation.1 | async-start | bytes 16384 | tf_op jit(solution)/shard_map/all_to_all | solution.py:138
  11.2 1.2 %convolution_convert_fusion.1 = bf16[128,2048]{1,0:T(8,128)(2,1)S(1)} fusion(bf16[32,2048]{1,0:T(8,128)(2,1)} %param.10, f32[128,32]{0,1:T(8,128)S(1)} %convert_reduce_fusion), kind=kOutput, calls=%fused_computation.7 | convolution fusion | flops 17043456 | bytes 671744 | tf_op jit(solution)/shard_map/dot_general | solution.py:128
  12.5 5.1 %all-to-all-done.1 = bf16[16,16,1]{1,2,0:T(2,128)(2,1)S(1)} async-done(((bf16[16,16,1]{1,2,0:T(2,128)(2,1)}), bf16[16,16,1]{1,2,0:T(2,128)(2,1)S(1)}, u32[]{:S(2)}, u32[]{:S(2)}) %all-to-all-start.1) | async-done | bytes 544 | tf_op jit(solution)/shard_map/all_to_all | solution.py:138
  17.6 1.1 %broadcast_in_dim.8 = bf16[8,2,16,2048]{3,2,1,0:T(8,128)(2,1)} broadcast(bf16[8,16,2048]{2,1,0:T(8,128)(2,1)S(1)} %bitcast.31), dimensions={0,2,3} | broadcast | bytes 1572864 | tf_op jit(solution)/shard_map/broadcast_in_dim | solution.py:134
  18.7 3.7 %all-to-all-start = ((bf16[16,16,2048]{2,1,0:T(8,128)(2,1)}), bf16[16,16,2048]{2,1,0:T(8,128)(2,1)S(1)}, u32[]{:S(2)}, u32[]{:S(2)}) async-start(bf16[16,16,2048]{2,1,0:T(8,128)(2,1)} %bitcast.1), calls=%async_computation | async-start | bytes 2097152 | tf_op jit(solution)/shard_map/all_to_all | solution.py:137
  22.5 3.9 %fusion.13 = f32[256,4096]{1,0:T(8,128)} fusion(f32[8,8,4096]{2,1,0:T(8,128)S(1)} %copy-done, s32[]{:T(128)S(6)} %select_n.31, f32[256]{0:T(256)S(1)} %sub.17), kind=kOutput, calls=%fused_computation.19 | convolution fusion | flops 100665344 | bytes 4326404 | tf_op jit(solution)/shard_map/dot_general | solution.py:22
  26.5 5.1 %fusion.16 = f32[256,7168]{1,0:T(8,128)} fusion(f32[8,7168]{1,0:T(8,128)S(1)} %bitcast.35, f32[256]{0:T(256)S(1)} %sub.17), kind=kOutput, calls=%fused_computation.23 | convolution fusion | flops 176162816 | bytes 7570432 | tf_op jit(solution)/shard_map/dot_general | solution.py:22
  31.6 13.6 %all-to-all-done = bf16[16,16,2048]{2,1,0:T(8,128)(2,1)S(1)} async-done(((bf16[16,16,2048]{2,1,0:T(8,128)(2,1)}), bf16[16,16,2048]{2,1,0:T(8,128)(2,1)S(1)}, u32[]{:S(2)}, u32[]{:S(2)}) %all-to-all-start) | async-done | bytes 1048608 | tf_op jit(solution)/shard_map/all_to_all | solution.py:137
  45.2 12.7 %convolution_multiply_fusion.1 = f32[256,3584]{1,0:T(8,128)} fusion(bf16[2048,3584]{1,0:T(8,128)(2,1)} %param.14, f32[256,7168]{1,0:T(8,128)} %fusion.16, bf16[256,2048]{1,0:T(8,128)(2,1)S(1)} %bitcast.33, f32[256,4096]{1,0:T(8,128)} %fusion.13), kind=kOutput, calls=%fused_computation.2 | convolution fusion | flops 3760586752 | bytes 25165824 | tf_op jit(solution)/shard_map/dot_general | solution.py:48
  57.9 16.9 %convolution_convert_fusion = bf16[256,2048]{1,0:T(8,128)(2,1)S(1)} fusion(bf16[3584,2048]{1,0:T(8,128)(2,1)} %param.16, bf16[2048,3584]{1,0:T(8,128)(2,1)} %param.15, f32[256,7168]{1,0:T(8,128)} %fusion.16, f32[256,3584]{1,0:T(8,128)} %convolution_multiply_fusion.1, bf16[256,2048]{1,0:T(8,128)(2,1)S(1)} %bitcast.34, f32[256,4096]{1,0:T(8,128)} %fusion.13), kind=kOutput, calls=%fused_computation.6 | convolution fusion | flops 7524712448 | bytes 40894464 | tf_op jit(solution)/shard_map/dot_general | solution.py:54
  74.7 0.2 convert.3
  75.1 0.7 collective-permute-start
  75.8 1.5 %collective-permute-done = bf16[16,8,2048]{2,1,0:T(8,128)(2,1)S(1)} collective-permute-done((bf16[16,8,2048]{2,1,0:T(8,128)(2,1)S(1)}, bf16[16,8,2048]{2,1,0:T(8,128)(2,1)S(1)}, u32[]{:S(2)}, u32[]{:S(2)}) %collective-permute-start) | collective-permute-done | bytes 524320 | tf_op jit(solution)/shard_map/ppermute | solution.py:18
  77.4 1.0 add_convert_fusion
  78.3 6.5 %all-to-all-start.2 = ((bf16[16,8,2048]{2,1,0:T(8,128)(2,1)}), bf16[16,8,2048]{2,1,0:T(8,128)(2,1)S(1)}, u32[]{:S(2)}, u32[]{:S(2)}) async-start(bf16[16,8,2048]{2,1,0:T(8,128)(2,1)} %add_convert_fusion), calls=%async_computation.2 | async-start | bytes 1048576 | tf_op jit(solution)/shard_map/all_to_all | solution.py:94
  85.2 13.9 %all-to-all-done.2 = bf16[16,8,2048]{2,1,0:T(8,128)(2,1)S(1)} async-done(((bf16[16,8,2048]{2,1,0:T(8,128)(2,1)}), bf16[16,8,2048]{2,1,0:T(8,128)(2,1)S(1)}, u32[]{:S(2)}, u32[]{:S(2)}) %all-to-all-start.2) | async-done | bytes 524320 | tf_op jit(solution)/shard_map/all_to_all | solution.py:94
  99.1 0.3 fusion.11
  99.4 0.4 fusion.2
  99.8 0.3 reshape.88
  100.1 1.3 %reduce_sum.32 = bf16[32,2048]{1,0:T(8,128)(2,1)} reduce(f32[32,2,2048]{2,1,0:T(2,128)S(1)} %reshape.88, f32[]{:T(128)} %constant.57.clone.1), dimensions={1}, to_apply=%region_3.4 | reduce | flops 65536 | bytes 655364 | tf_op jit(solution)/shard_map/reduce_sum | solution.py:161
  (30 shorter events, 1.5 us)
Async XLA Ops:
  0.0 22.5 %copy-start = (f32[8,8,4096]{2,1,0:T(8,128)S(1)}, f32[8,8,4096]{2,1,0:T(8,128)}, u32[]{:S(2)}) copy-start(f32[8,8,4096]{2,1,0:T(8,128)} %param.17) | copy-start | bytes 3145732
  0.0 22.4 %copy-start.3 = (f32[8,2,3584]{2,1,0:T(2,128)S(1)}, f32[8,2,3584]{2,1,0:T(2,128)}, u32[]{:S(2)}) copy-start(f32[8,2,3584]{2,1,0:T(2,128)} %param.18) | copy-start | bytes 688132
  3.8 13.8 %all-to-all-start.1 = ((bf16[16,16,1]{1,2,0:T(2,128)(2,1)}), bf16[16,16,1]{1,2,0:T(2,128)(2,1)S(1)}, u32[]{:S(2)}, u32[]{:S(2)}) async-start(bf16[16,16,1]{1,2,0:T(2,128)(2,1)} %copy.36), calls=%async_computation.1 | async-start | bytes 16384 | tf_op jit(solution)/shard_map/all_to_all | solution.py:138
  18.7 26.5 %all-to-all-start = ((bf16[16,16,2048]{2,1,0:T(8,128)(2,1)}), bf16[16,16,2048]{2,1,0:T(8,128)(2,1)S(1)}, u32[]{:S(2)}, u32[]{:S(2)}) async-start(bf16[16,16,2048]{2,1,0:T(8,128)(2,1)} %bitcast.1), calls=%async_computation | async-start | bytes 2097152 | tf_op jit(solution)/shard_map/all_to_all | solution.py:137
  75.0 9.9 %copy-start.5 = (f32[32,2]{0,1:T(2,128)S(1)}, f32[32,2]{0,1:T(2,128)}, u32[]{:S(2)}) copy-start(f32[32,2]{0,1:T(2,128)} %param.13) | copy-start | bytes 772
  75.0 10.1 %copy-start.4 = (s32[32]{0:T(128)S(1)}, s32[32]{0:T(128)}, u32[]{:S(2)}) copy-start(s32[32]{0:T(128)} %param.12) | copy-start | bytes 388
  75.0 24.4 %copy-start.2 = (f32[8,8,2048]{2,1,0:T(8,128)S(1)}, f32[8,8,2048]{2,1,0:T(8,128)}, u32[]{:S(2)}) copy-start(f32[8,8,2048]{2,1,0:T(8,128)} %param.19) | copy-start | bytes 1572868
  75.0 26.5 %copy-start.1 = (f32[8,8,4096]{2,1,0:T(8,128)S(1)}, f32[8,8,4096]{2,1,0:T(8,128)}, u32[]{:S(2)}) copy-start(f32[8,8,4096]{2,1,0:T(8,128)} %param.17) | copy-start | bytes 3145732
  75.1 2.3 %collective-permute-start = (bf16[16,8,2048]{2,1,0:T(8,128)(2,1)S(1)}, bf16[16,8,2048]{2,1,0:T(8,128)(2,1)S(1)}, u32[]{:S(2)}, u32[]{:S(2)}) collective-permute-start(bf16[16,8,2048]{2,1,0:T(8,128)(2,1)S(1)} %select_convert_fusion), channel_id=1, source_target_pairs={{0,1},{1,0},{2,3},{3,2},{4,5},{5,4},{6,7},{7,6},{8,9},{9,8},{10,11... | collective-permute-start | bytes 1572872 | tf_op jit(solution)/shard_map/ppermute | solution.py:18
  78.3 20.7 %all-to-all-start.2 = ((bf16[16,8,2048]{2,1,0:T(8,128)(2,1)}), bf16[16,8,2048]{2,1,0:T(8,128)(2,1)S(1)}, u32[]{:S(2)}, u32[]{:S(2)}) async-start(bf16[16,8,2048]{2,1,0:T(8,128)(2,1)} %add_convert_fusion), calls=%async_computation.2 | async-start | bytes 1048576 | tf_op jit(solution)/shard_map/all_to_all | solution.py:94
where the time goes:
time: 102 us; the launch traced here: 101 us
  matrix products  41.3 us (40%)
  waiting for transfers between devices  34.1 us (33%)
  starting transfers between devices  18.3 us (18%)
  other arithmetic  3.79 us (4%)
  local copies, waits for them, and re-layouts  3.78 us (4%)
    dot_general x1, matrix products, expert_rows(): jnp.dot(hidden, down_weight, preferred_element_type=jnp.float32)  16.9 us
    all_to_all x1, waiting for transfers between devices, send_back(): lax.all_to_all(held.astype(jnp.bfloat16), 'expert', split_axis=0, concat_...  13.9 us
    all_to_all x1, waiting for transfers between devices, per_device(): lax.all_to_all(rows_out, 'expert', split_axis=0, concat_axis=0, tiled=True)  13.6 us
    dot_general x1, matrix products, expert_rows(): gate = jnp.dot(gate_in, gate_weight, preferred_element_type=jnp.float32)  12.7 us
    dot_general x3, matrix products, lookup(): jnp.dot(select, table, precision=lax.Precision.HIGHEST, preferred_element...  9.45 us
    all_to_all x1, starting transfers between devices, per_device(): lax.all_to_all(member_out, 'expert', split_axis=0, concat_axis=0, tiled=T...  7.41 us
    all_to_all x1, starting transfers between devices, send_back(): lax.all_to_all(held.astype(jnp.bfloat16), 'expert', split_axis=0, concat_...  6.45 us
    all_to_all x1, waiting for transfers between devices, per_device(): lax.all_to_all(member_out, 'expert', split_axis=0, concat_axis=0, tiled=T...  5.13 us
  transfers between devices with their start and end apart: 4, of which 4 were waited for; matrix products, arithmetic and copies ran while one was open for 11% of the time, Pallas kernels for 0%

commit v1 on v0

v1 whole, which is shorter than its diff:
```python
import functools

import jax
import jax.numpy as jnp
from jax import lax
from jax.experimental import pallas as pl
from jax.experimental.pallas import tpu as pltpu
from jax.sharding import PartitionSpec as P

EXPERTS = 8
CAP = 16
LANES = 128
CHUNKS = 4
BF16 = jnp.bfloat16
F32 = jnp.float32


def tile_of(size):
    for tile in (512, 256, 128):
        if size % tile == 0:
            return tile
    return size


def parts_of(table):
    high = table.astype(BF16).astype(F32)
    rest = table - high
    mid = rest.astype(BF16).astype(F32)
    low = (rest - mid).astype(BF16).astype(F32)
    return high, mid, low


def kernel(
    n,
    tok_ref,
    ids_ref,
    mem_ref,
    cw_ref,
    hidf_ref,
    wg_hbm,
    wu_hbm,
    wd_hbm,
    inf_hbm,
    outf_hbm,
    o_ref,
    wg,
    wu,
    wd,
    inf,
    outf,
    tab_in,
    tab_hid,
    tab_out,
    send,
    recv,
    gate_in,
    up_in,
    hidden,
    psend,
    precv,
    osend,
    home,
    placing,
    wsem,
    fsem,
    dsend,
    drecv,
    psems,
    precs,
    hsend,
    hrecv,
    xsend,
    xrecv,
):
    split = n // EXPERTS
    toks, width = tok_ref.shape
    units = wg.shape[1]
    members = inf.shape[0]
    seg = EXPERTS * CAP
    me = lax.axis_index("expert")
    own = lax.div(me, split)
    part = lax.rem(me, split)

    def expert_at(k):
        return lax.rem(own + (k + EXPERTS) % EXPERTS, EXPERTS)

    def part_at(j):
        return lax.rem(part + (j + split) % split, split)

    def far(k):
        return {"expert": expert_at(k) * split + part}

    def near(j):
        return {"expert": own * split + part_at(j)}

    def rows(index, count=CAP):
        return pl.ds(pl.multiple_of(index * count, count), count)

    barrier = pltpu.get_barrier_semaphore()
    for k in range(1, EXPERTS):
        pl.semaphore_signal(barrier, inc=1, device_id=far(k), device_id_type=pl.DeviceIdType.MESH)
    for j in range(1, split):
        pl.semaphore_signal(barrier, inc=1, device_id=near(j), device_id_type=pl.DeviceIdType.MESH)

    loads = [
        pltpu.make_async_copy(inf_hbm.at[own], inf, fsem.at[0]),
        pltpu.make_async_copy(outf_hbm.at[own], outf, fsem.at[1]),
    ]
    weights = []
    for index, (src, dst) in enumerate(((wg_hbm, wg), (wu_hbm, wu), (wd_hbm, wd))):
        step = src.shape[0] // CHUNKS
        weights.append(
            [
                pltpu.make_async_copy(
                    src.at[pl.ds(c * step, step)], dst.at[pl.ds(c * step, step)], wsem.at[index, c]
                )
                for c in range(CHUNKS)
            ]
        )
    for copy in loads + weights[0] + weights[1] + weights[2]:
        copy.start()

    ids = ids_ref[...]
    lane = lax.broadcasted_iota(jnp.int32, (toks, seg), 1)
    lane_expert = lax.shift_right_logical(lane, CAP.bit_length() - 1)
    lane_slot = lax.bitwise_and(lane, CAP - 1)
    hit0 = ids[:, 0:1] == lane_expert
    hit1 = ids[:, 1:2] == lane_expert
    named = jnp.where(hit0 | hit1, 1.0, 0.0)
    down_i = lax.broadcasted_iota(jnp.int32, (toks, toks), 0)
    across = lax.broadcasted_iota(jnp.int32, (toks, toks), 1)
    earlier = jnp.where(across < down_i, 1.0, 0.0)
    rank = jnp.dot(earlier.astype(BF16), named.astype(BF16), preferred_element_type=F32)
    placed = jnp.where(rank == lane_slot.astype(F32), named, 0.0)
    placing[...] = placed.astype(BF16)
    member = jnp.sum(
        jnp.where(across == down_i, jnp.broadcast_to(mem_ref[...].astype(F32), (toks, toks)), 0.0),
        axis=1,
        keepdims=True,
    )
    col = lax.broadcasted_iota(jnp.int32, (toks, LANES), 1)
    col_member = lax.rem(col, members).astype(F32)
    onehot = jnp.where((col < 3 * members) & (col_member == member), 1.0, 0.0)
    cw = cw_ref[...]

    def gather(which, data):
        return lax.dot_general(
            which.astype(BF16), data.astype(BF16), (((0,), (0,)), ((), ())), preferred_element_type=F32
        )

    meta_rows = jnp.zeros((seg, LANES), F32)
    for route, hit in ((0, hit0), (1, hit1)):
        meta = onehot
        for spot, piece in enumerate(parts_of(cw[:, route : route + 1])):
            meta = jnp.where(col == 3 * members + spot, piece, meta)
        meta_rows = meta_rows + gather(jnp.where(hit, placed, 0.0), meta)
    send[:, width:] = meta_rows.astype(BF16)
    wide = tile_of(width)
    for t in range(width // wide):
        cols = slice(t * wide, (t + 1) * wide)
        send[:, cols] = gather(placed, tok_ref[:, cols]).astype(BF16)

    pl.semaphore_wait(barrier, EXPERTS - 1 + split - 1)

    def direct(k):
        return pltpu.make_async_remote_copy(
            src_ref=send.at[rows(expert_at(k))],
            dst_ref=recv.at[rows(part * EXPERTS + own)],
            send_sem=dsend.at[k],
            recv_sem=drecv.at[k],
            device_id=far(k),
            device_id_type=pl.DeviceIdType.MESH,
        )

    def landed(k, j):
        return rows(part_at(-j) * EXPERTS + expert_at(-k))

    def handed(k, j):
        return pltpu.make_async_remote_copy(
            src_ref=recv.at[landed(k, 0)] if k else send.at[rows(own)],
            dst_ref=recv.at[landed(k, 0)],
            send_sem=xsend.at[k, j],
            recv_sem=xrecv.at[k, j],
            device_id=near(j),
            device_id_type=pl.DeviceIdType.MESH,
        )

    for k in range(1, EXPERTS):
        direct(k).start()
    for j in range(1, split):
        handed(0, j).start()
    recv[landed(0, 0), :] = send[rows(own), :]

    for copy in loads:
        copy.wait()
    for tab in (tab_in, tab_hid, tab_out):
        tab[...] = jnp.zeros(tab.shape, tab.dtype)

    def fill(tab, at, table):
        high, mid, low = parts_of(table)
        pad = jnp.zeros_like(high)
        tab[0 : 4 * members, at : at + table.shape[1]] = jnp.concatenate(
            [high, mid, low, pad], axis=0
        ).astype(BF16)

    for t in range(2 * width // wide):
        fill(tab_in, t * wide, inf[:, t * wide : (t + 1) * wide])
    for t in range(width // wide):
        fill(tab_out, t * wide, outf[:, t * wide : (t + 1) * wide])
    tile = tile_of(units)
    for g in range(2):
        for t in range(units // tile):
            fill(tab_hid, g * units + t * tile, hidf_ref[:, g, t * tile : (t + 1) * tile])

    for k in range(1, EXPERTS):
        pltpu.make_async_remote_copy(
            src_ref=recv.at[landed(k, 0)],
            dst_ref=recv.at[landed(k, 0)],
            send_sem=dsend.at[k],
            recv_sem=drecv.at[k],
            device_id=far(k),
            device_id_type=pl.DeviceIdType.MESH,
        ).wait_recv()
        for j in range(1, split):
            handed(k, j).start()
    for k in range(EXPERTS):
        for j in range(1, split):
            pltpu.make_async_remote_copy(
                src_ref=recv.at[landed(k, j)],
                dst_ref=recv.at[landed(k, j)],
                send_sem=xsend.at[k, j],
                recv_sem=xrecv.at[k, j],
                device_id=near(j),
                device_id_type=pl.DeviceIdType.MESH,
            ).wait_recv()

    meta = recv[:, width:]

    for t in range(width // wide):
        cols = slice(t * wide, (t + 1) * wide)
        data = recv[:, cols].astype(F32)
        scale = jnp.dot(meta, tab_in[:, cols], preferred_element_type=F32)
        gate_in[:, cols] = (data * scale).astype(BF16)
        cols_up = slice(width + t * wide, width + (t + 1) * wide)
        scale = jnp.dot(meta, tab_in[:, cols_up], preferred_element_type=F32)
        up_in[:, cols] = (data * scale).astype(BF16)

    for copy in weights[0] + weights[1]:
        copy.wait()

    def hidden_tile(t, carry):
        cols = pl.ds(pl.multiple_of(t * tile, tile), tile)
        cols_up = pl.ds(pl.multiple_of(units + t * tile, LANES), tile)
        gate = jnp.dot(gate_in[...], wg[:, cols], preferred_element_type=F32)
        gate = gate * jnp.dot(recv[:, width:], tab_hid[:, cols], preferred_element_type=F32)
        up = jnp.dot(up_in[...], wu[:, cols], preferred_element_type=F32)
        up = up * jnp.dot(recv[:, width:], tab_hid[:, cols_up], preferred_element_type=F32)
        hidden[:, cols] = (gate / (1.0 + jnp.exp(-gate)) * up).astype(BF16)
        return carry

    lax.fori_loop(0, units // tile, hidden_tile, 0)

    for copy in weights[2]:
        copy.wait()

    tiles, _, out_tile = psend.shape
    seg_meta = recv[rows(part, seg), width:]
    seg_col = lax.broadcasted_iota(jnp.int32, (seg, LANES), 1)
    weight = jnp.sum(
        jnp.where((seg_col >= 3 * members) & (seg_col < 3 * members + 3), seg_meta.astype(F32), 0.0),
        axis=1,
        keepdims=True,
    )

    def share(t, j):
        return pltpu.make_async_remote_copy(
            src_ref=psend.at[t, rows(part_at(j), seg)],
            dst_ref=precv.at[t, j],
            send_sem=psems.at[t, j],
            recv_sem=precs.at[t, j],
            device_id=near(j),
            device_id_type=pl.DeviceIdType.MESH,
        )

    def back(t, k):
        return pltpu.make_async_remote_copy(
            src_ref=osend.at[t, rows(expert_at(k))],
            dst_ref=home.at[t, rows(own)],
            send_sem=hsend.at[t, k],
            recv_sem=hrecv.at[t, k],
            device_id=far(k),
            device_id_type=pl.DeviceIdType.MESH,
        )

    def finish(t):
        total = psend[t, rows(part, seg), :].astype(F32)
        for j in range(1, split):
            share(t, j).wait_recv()
            total = total + precv[t, j].astype(F32)
        cols = slice(t * out_tile, (t + 1) * out_tile)
        scale = jnp.dot(seg_meta, tab_out[:, cols], preferred_element_type=F32)
        osend[t] = (total * scale * weight).astype(BF16)
        for k in range(1, EXPERTS):
            back(t, k).start()
        home[t, rows(own), :] = osend[t, rows(own), :]

    for t in range(tiles):
        cols = slice(t * out_tile, (t + 1) * out_tile)
        psend[t] = jnp.dot(hidden[...], wd[:, cols], preferred_element_type=F32).astype(BF16)
        for j in range(1, split):
            share(t, j).start()
        if t > 0:
            finish(t - 1)
    finish(tiles - 1)

    for t in range(tiles):
        cols = slice(t * out_tile, (t + 1) * out_tile)
        for k in range(1, EXPERTS):
            back(t, k).wait_recv()
        o_ref[:, cols] = jnp.dot(placing[...], home[t], preferred_element_type=F32).astype(BF16)

    for k in range(1, EXPERTS):
        direct(k).wait_send()
    for k in range(EXPERTS):
        for j in range(1, split):
            handed(k, j).wait_send()
    for t in range(tiles):
        for j in range(1, split):
            share(t, j).wait_send()
        for k in range(1, EXPERTS):
            back(t, k).wait_send()


def per_device(
    tokens,
    expert_ids,
    member_ids,
    combine_weights,
    gate_weight,
    up_weight,
    down_weight,
    input_factors,
    hidden_factors,
    output_factors,
):
    n = lax.axis_size("expert")
    split = n // EXPERTS
    toks, width = tokens.shape
    units = gate_weight.shape[1]
    members = input_factors.shape[1]
    seg = EXPERTS * CAP
    all_rows = n * CAP
    out_tile = tile_of(width)
    tiles = width // out_tile
    vmem = pl.BlockSpec(memory_space=pltpu.VMEM)
    hbm = pl.BlockSpec(memory_space=pl.ANY)
    dma = pltpu.SemaphoreType.DMA
    return pl.pallas_call(
        functools.partial(kernel, n),
        out_shape=jax.ShapeDtypeStruct((toks, width), BF16),
        in_specs=[vmem] * 5 + [hbm] * 5,
        out_specs=vmem,
        scratch_shapes=[
            pltpu.VMEM((width, units), BF16),
            pltpu.VMEM((width, units), BF16),
            pltpu.VMEM((units, width), BF16),
            pltpu.VMEM((members, 2 * width), F32),
            pltpu.VMEM((members, width), F32),
            pltpu.VMEM((LANES, 2 * width), BF16),
            pltpu.VMEM((LANES, 2 * units), BF16),
            pltpu.VMEM((LANES, width), BF16),
            pltpu.VMEM((seg, width + LANES), BF16),
            pltpu.VMEM((all_rows, width + LANES), BF16),
            pltpu.VMEM((all_rows, width), BF16),
            pltpu.VMEM((all_rows, width), BF16),
            pltpu.VMEM((all_rows, units), BF16),
            pltpu.VMEM((tiles, all_rows, out_tile), BF16),
            pltpu.VMEM((tiles, split, seg, out_tile), BF16),
            pltpu.VMEM((tiles, seg, out_tile), BF16),
            pltpu.VMEM((tiles, seg, out_tile), BF16),
            pltpu.VMEM((toks, seg), BF16),
            dma((3, CHUNKS)),
            dma((2,)),
            dma((EXPERTS,)),
            dma((EXPERTS,)),
            dma((tiles, split)),
            dma((tiles, split)),
            dma((tiles, EXPERTS)),
            dma((tiles, EXPERTS)),
            dma((EXPERTS, split)),
            dma((EXPERTS, split)),
        ],
        compiler_params=pltpu.CompilerParams(
            collective_id=0, has_side_effects=True, vmem_limit_bytes=67043328
        ),
        name="moe_step",
    )(
        tokens,
        expert_ids,
        member_ids.reshape(1, toks),
        combine_weights,
        hidden_factors,
        gate_weight,
        up_weight,
        down_weight,
        input_factors,
        output_factors,
    )


def solution(mesh):
    in_specs = (
        P(("groups", "expert"), None),
        P(("groups", "expert"), None),
        P(("groups", "expert")),
        P(("groups", "expert"), None),
        P(None, "expert"),
        P(None, "expert"),
        P("expert", None),
        P(),
        P(None, None, "expert"),
        P(),
    )
    out_specs = P(("groups", "expert"), None)
    return jax.shard_map(
        per_device, mesh=mesh, in_specs=in_specs, out_specs=out_specs, check_vma=False
    )
```

time: 102 us -> 52.6 us (0.52)
  Pallas kernels: 0 us -> 48.1 us
  matrix products: 41.3 us -> 0 us
  waiting for transfers between devices: 34.1 us -> 0 us
  starting transfers between devices: 18.3 us -> 0 us
  other arithmetic: 3.79 us -> 0 us
    pallas_call x0 -> x1, Pallas kernels: none -> 48.1 us  [per_device(): pl.pallas_call(functools.partial(kernel, n), out_shape=jax.ShapeDtypeStru...]
    dot_general x8 -> x0, matrix products: 41.3 us -> none  [the longest x1 16.9 us: expert_rows(): jnp.dot(hidden, down_weight, preferred_element_type=jnp.float32)]
    all_to_all x3 -> x0, waiting for transfers between devices: 32.6 us -> none  [the longest x1 13.9 us: send_back(): lax.all_to_all(held.astype(jnp.bfloat16), 'expert', split_axis=0, concat_...]
    all_to_all x3 -> x0, starting transfers between devices: 17.5 us -> none  [the longest x1 7.41 us: per_device(): lax.all_to_all(member_out, 'expert', split_axis=0, concat_axis=0, tiled=T...]
    unnamed x15 -> x3, local copies, waits for them, and re-layouts: 1.03 us -> 4.29 us
    broadcast_in_dim x4 -> x0, local copies, waits for them, and re-layouts: 1.79 us -> none  [the longest x1 1.09 us: per_device(): rows_out = jnp.repeat(send_rows.reshape(EXPERTS, CAP, width), split, axis=0)]
    reduce_sum x3 -> x0, other arithmetic: 1.6 us -> none  [the longest x1 1.34 us: per_device(): return weighted.reshape(tok_count, 2, width).sum(1).astype(jnp.bfloat16)]
    ppermute x1 -> x0, waiting for transfers between devices: 1.54 us -> none  [swapped(): return lax.ppermute(block, axis, route)]
  transfers between devices with their start and end apart: 4 -> 0, of which waited for: 4 -> 0; matrix products, arithmetic and copies ran while one was open for 11% -> 0% of each run, Pallas kernels for 0% -> 0%
where the time goes in v1:
time: 52.6 us; the launch traced here: 52.4 us
  Pallas kernels  48.1 us (91%)
  local copies, waits for them, and re-layouts  4.29 us (8%)
    pallas_call x1, Pallas kernels, per_device(): pl.pallas_call(functools.partial(kernel, n), out_shape=jax.ShapeDtypeStru...  48.1 us
    unnamed x3, local copies, waits for them, and re-layouts  4.29 us

profile of v1, /device:TPU:0, one launch (start us, length us, event | category | flops | bytes accessed | tf_op | source)
XLA Modules:
  0.0 52.4 jit_solution(330258375748161356)
XLA Ops:
  0.0 1.4 %copy.11.ids_ref = s32[32,2]{1,0:T(8,128)} copy(s32[32,2]{0,1:T(2,128)} %param.11) | data formatting | bytes 512 | tf_op args[1]
  1.4 1.4 %copy.12.cw_ref = f32[32,2]{1,0:T(8,128)} copy(f32[32,2]{0,1:T(2,128)} %param.13) | data formatting | bytes 512 | tf_op args[3]
  2.7 48.1 %moe_step.1 = bf16[32,2048]{1,0:T(8,128)(2,1)} custom-call(bf16[32,2048]{1,0:T(8,128)(2,1)} %tok_ref.1, s32[32,2]{1,0:T(8,128)} %copy.11.ids_ref, s32[1,32]{1,0:T(1,128)} %bitcast.1, f32[32,2]{1,0:T(8,128)} %copy.12.cw_ref, f32[8,2,3584]{2,1,0:T(2,128)} %hidf_ref.1, bf16[2048,3584]{1,0:T(8,128)(2,1)} %wg_hbm.1, bf16[2048,3584]{1,0:T(8,128)(2,1)} %wu_hbm.1, ...), custom_call_target="tpu_custom_call" | custom-call | tf_op jit(solution)/shard_map/moe_step/pallas_call | solution.py:358
  50.8 1.6 %copy.14 = bf16[32,2048]{1,0:T(8,128)(2,1)} copy(bf16[32,2048]{1,0:T(8,128)(2,1)} %moe_step.1) | data formatting | bytes 262144

commit v2 on v1

v2 whole, which is shorter than its diff:
```python
import functools

import jax
import jax.numpy as jnp
from jax import lax
from jax.experimental import pallas as pl
from jax.experimental.pallas import tpu as pltpu
from jax.sharding import PartitionSpec as P

EXPERTS = 8
CAP = 16
LANES = 128
CHUNKS = 4
BATCHES = ((0, 1, 4, 6), (2, 3, 5, 7))
PLACE = {k: (b, i) for b, ks in enumerate(BATCHES) for i, k in enumerate(ks)}
BF16 = jnp.bfloat16
F32 = jnp.float32


def tile_of(size):
    for tile in (512, 256, 128):
        if size % tile == 0:
            return tile
    return size


def parts_of(table):
    high = table.astype(BF16).astype(F32)
    rest = table - high
    mid = rest.astype(BF16).astype(F32)
    low = (rest - mid).astype(BF16).astype(F32)
    return high, mid, low


def kernel(
    n,
    ids_ref,
    mem_ref,
    cw_ref,
    tok_hbm,
    hidf_hbm,
    wg_hbm,
    wu_hbm,
    wd_hbm,
    inf_hbm,
    outf_hbm,
    o_ref,
    tok_ref,
    hidf_ref,
    wg,
    wu,
    wd,
    inf,
    outf,
    tab_in,
    tab_hid,
    tab_out,
    send,
    recv,
    gate_in,
    up_in,
    hidden,
    psend,
    precv,
    osend,
    home,
    placing,
    wsem,
    fsem,
    dsend,
    drecv,
    psems,
    precs,
    hsend,
    hrecv,
    xsend,
    xrecv,
):
    split = n // EXPERTS
    toks, width = tok_ref.shape
    units = wg.shape[1]
    members = inf.shape[0]
    seg = EXPERTS * CAP
    me = lax.axis_index("expert")
    own = lax.div(me, split)
    part = lax.rem(me, split)

    def expert_at(k):
        return lax.bitwise_xor(own, k)

    def part_at(j):
        return lax.rem(part + (j + split) % split, split)

    def far(k):
        return {"expert": expert_at(k) * split + part}

    def near(j):
        return {"expert": own * split + part_at(j)}

    def rows(index, count=CAP):
        return pl.ds(pl.multiple_of(index * count, count), count)

    barrier = pltpu.get_barrier_semaphore()
    for k in range(1, EXPERTS):
        pl.semaphore_signal(barrier, inc=1, device_id=far(k), device_id_type=pl.DeviceIdType.MESH)
    for j in range(1, split):
        pl.semaphore_signal(barrier, inc=1, device_id=near(j), device_id_type=pl.DeviceIdType.MESH)

    loads = [
        pltpu.make_async_copy(inf_hbm.at[own], inf, fsem.at[0]),
        pltpu.make_async_copy(hidf_hbm, hidf_ref, fsem.at[2]),
        pltpu.make_async_copy(outf_hbm.at[own], outf, fsem.at[1]),
    ]
    weights = []
    for index, (src, dst) in enumerate(((wg_hbm, wg), (wu_hbm, wu), (wd_hbm, wd))):
        step = src.shape[0] // CHUNKS
        weights.append(
            [
                pltpu.make_async_copy(
                    src.at[pl.ds(c * step, step)], dst.at[pl.ds(c * step, step)], wsem.at[index, c]
                )
                for c in range(CHUNKS)
            ]
        )
    tok_load = pltpu.make_async_copy(tok_hbm, tok_ref, fsem.at[3])
    for copy in [tok_load] + loads + weights[0] + weights[1]:
        copy.start()

    down_i = lax.broadcasted_iota(jnp.int32, (toks, toks), 0)
    across = lax.broadcasted_iota(jnp.int32, (toks, toks), 1)

    def column(row):
        spread = jnp.broadcast_to(row.astype(F32), (toks, toks))
        return jnp.sum(jnp.where(across == down_i, spread, 0.0), axis=1, keepdims=True)

    lane = lax.broadcasted_iota(jnp.int32, (toks, seg), 1)
    lane_expert = lax.shift_right_logical(lane, CAP.bit_length() - 1)
    lane_slot = lax.bitwise_and(lane, CAP - 1)
    hit0 = column(ids_ref[0:1, :]) == lane_expert.astype(F32)
    hit1 = column(ids_ref[1:2, :]) == lane_expert.astype(F32)
    named = jnp.where(hit0 | hit1, 1.0, 0.0)
    earlier = jnp.where(across < down_i, 1.0, 0.0)
    rank = jnp.dot(earlier.astype(BF16), named.astype(BF16), preferred_element_type=F32)
    placed = jnp.where(rank == lane_slot.astype(F32), named, 0.0)
    placing[...] = placed.astype(BF16)
    member = column(mem_ref[...])
    col = lax.broadcasted_iota(jnp.int32, (toks, LANES), 1)
    col_member = lax.rem(col, members).astype(F32)
    onehot = jnp.where((col < 3 * members) & (col_member == member), 1.0, 0.0)

    def gather(which, data):
        return lax.dot_general(
            which.astype(BF16), data.astype(BF16), (((0,), (0,)), ((), ())), preferred_element_type=F32
        )

    meta_rows = jnp.zeros((seg, LANES), F32)
    for route, hit in ((0, hit0), (1, hit1)):
        meta = onehot
        for spot, piece in enumerate(parts_of(column(cw_ref[route : route + 1, :]))):
            meta = jnp.where(col == 3 * members + spot, piece, meta)
        meta_rows = meta_rows + gather(jnp.where(hit, placed, 0.0), meta)
    send[:, width:] = meta_rows.astype(BF16)
    wide = tile_of(width)
    tok_load.wait()
    for t in range(width // wide):
        cols = slice(t * wide, (t + 1) * wide)
        send[:, cols] = gather(placed, tok_ref[:, cols]).astype(BF16)

    pl.semaphore_wait(barrier, EXPERTS - 1 + split - 1)

    def direct(k):
        return pltpu.make_async_remote_copy(
            src_ref=send.at[rows(expert_at(k))],
            dst_ref=recv.at[landed(k, 0)],
            send_sem=dsend.at[k],
            recv_sem=drecv.at[k],
            device_id=far(k),
            device_id_type=pl.DeviceIdType.MESH,
        )

    def landed(k, j):
        batch, slot = PLACE[k]
        each = len(BATCHES[batch])
        return rows(batch * split * each + part_at(-j) * each + slot)

    def handed(k, j):
        return pltpu.make_async_remote_copy(
            src_ref=recv.at[landed(k, 0)] if k else send.at[rows(own)],
            dst_ref=recv.at[landed(k, 0)],
            send_sem=xsend.at[k, j],
            recv_sem=xrecv.at[k, j],
            device_id=near(j),
            device_id_type=pl.DeviceIdType.MESH,
        )

    for k in BATCHES[0] + BATCHES[1]:
        if k:
            direct(k).start()
    for j in range(1, split):
        handed(0, j).start()
    recv[landed(0, 0), :] = send[rows(own), :]

    for copy in loads:
        copy.wait()
    for tab in (tab_in, tab_hid, tab_out):
        tab[...] = jnp.zeros(tab.shape, tab.dtype)

    def fill(tab, at, table):
        high, mid, low = parts_of(table)
        pad = jnp.zeros_like(high)
        tab[0 : 4 * members, at : at + table.shape[1]] = jnp.concatenate(
            [high, mid, low, pad], axis=0
        ).astype(BF16)

    for t in range(2 * width // wide):
        fill(tab_in, t * wide, inf[:, t * wide : (t + 1) * wide])
    for t in range(width // wide):
        fill(tab_out, t * wide, outf[:, t * wide : (t + 1) * wide])
    tile = tile_of(units)
    for g in range(2):
        for t in range(units // tile):
            fill(tab_hid, g * units + t * tile, hidf_ref[:, g, t * tile : (t + 1) * tile])

    for copy in weights[2]:
        copy.start()

    def hand_on(ks):
        for k in ks:
            if k:
                pltpu.make_async_remote_copy(
                    src_ref=recv.at[landed(k, 0)],
                    dst_ref=recv.at[landed(k, 0)],
                    send_sem=dsend.at[k],
                    recv_sem=drecv.at[k],
                    device_id=far(k),
                    device_id_type=pl.DeviceIdType.MESH,
                ).wait_recv()
                for j in range(1, split):
                    handed(k, j).start()

    tiles, _, out_tile = home.shape
    batch_rows = recv.shape[0] // len(BATCHES)
    share_rows = batch_rows // split

    def scale_inputs(b):
        for k in BATCHES[b]:
            for j in range(1, split):
                pltpu.make_async_remote_copy(
                    src_ref=recv.at[landed(k, j)],
                    dst_ref=recv.at[landed(k, j)],
                    send_sem=xsend.at[k, j],
                    recv_sem=xrecv.at[k, j],
                    device_id=near(j),
                    device_id_type=pl.DeviceIdType.MESH,
                ).wait_recv()
        mine = slice(b * batch_rows, (b + 1) * batch_rows)
        meta = recv[mine, width:]
        for t in range(width // wide):
            cols = slice(t * wide, (t + 1) * wide)
            data = recv[mine, cols].astype(F32)
            scale = jnp.dot(meta, tab_in[:, cols], preferred_element_type=F32)
            gate_in[:, cols] = (data * scale).astype(BF16)
            cols_up = slice(width + t * wide, width + (t + 1) * wide)
            scale = jnp.dot(meta, tab_in[:, cols_up], preferred_element_type=F32)
            up_in[:, cols] = (data * scale).astype(BF16)

    def hidden_units(b):
        mine = slice(b * batch_rows, (b + 1) * batch_rows)

        def hidden_tile(t, carry):
            cols = pl.ds(pl.multiple_of(t * tile, tile), tile)
            cols_up = pl.ds(pl.multiple_of(units + t * tile, LANES), tile)
            meta = recv[mine, width:]
            gate = jnp.dot(gate_in[...], wg[:, cols], preferred_element_type=F32)
            gate = gate * jnp.dot(meta, tab_hid[:, cols], preferred_element_type=F32)
            up = jnp.dot(up_in[...], wu[:, cols], preferred_element_type=F32)
            up = up * jnp.dot(meta, tab_hid[:, cols_up], preferred_element_type=F32)
            hidden[:, cols] = (gate / (1.0 + jnp.exp(-gate)) * up).astype(BF16)
            return carry

        lax.fori_loop(0, units // tile, hidden_tile, 0)

    def share(b, t, j):
        return pltpu.make_async_remote_copy(
            src_ref=psend.at[b, t, rows(part_at(j), share_rows)],
            dst_ref=precv.at[b, t, j],
            send_sem=psems.at[b, t, j],
            recv_sem=precs.at[b, t, j],
            device_id=near(j),
            device_id_type=pl.DeviceIdType.MESH,
        )

    def back(t, k):
        batch, slot = PLACE[k]
        return pltpu.make_async_remote_copy(
            src_ref=osend.at[batch, t, pl.ds(slot * CAP, CAP)],
            dst_ref=home.at[t, rows(own)],
            send_sem=hsend.at[t, k],
            recv_sem=hrecv.at[t, k],
            device_id=far(k),
            device_id_type=pl.DeviceIdType.MESH,
        )

    def down_tile(b, t):
        cols = slice(t * out_tile, (t + 1) * out_tile)
        psend[b, t] = jnp.dot(hidden[...], wd[:, cols], preferred_element_type=F32).astype(BF16)
        for j in range(1, split):
            share(b, t, j).start()

    def finish(b, t):
        first = len(BATCHES[0]) * CAP * split * b
        meta = recv[pl.ds(pl.multiple_of(first + part * share_rows, CAP), share_rows), width:]
        spot = lax.broadcasted_iota(jnp.int32, (share_rows, LANES), 1)
        weight = jnp.sum(
            jnp.where((spot >= 3 * members) & (spot < 3 * members + 3), meta.astype(F32), 0.0),
            axis=1,
            keepdims=True,
        )
        total = psend[b, t, rows(part, share_rows), :].astype(F32)
        for j in range(1, split):
            share(b, t, j).wait_recv()
            total = total + precv[b, t, j].astype(F32)
        cols = slice(t * out_tile, (t + 1) * out_tile)
        scale = jnp.dot(meta, tab_out[:, cols], preferred_element_type=F32)
        value = (total * scale * weight).astype(BF16)
        osend[b, t] = value
        for slot, k in enumerate(BATCHES[b]):
            if k:
                back(t, k).start()
            else:
                home[t, rows(own), :] = value[slot * CAP : (slot + 1) * CAP]

    hand_on(BATCHES[0])
    scale_inputs(0)
    for copy in weights[0] + weights[1]:
        copy.wait()
    hidden_units(0)
    hand_on(BATCHES[1][:2])
    for copy in weights[2]:
        copy.wait()
    for t in range(tiles):
        down_tile(0, t)
        if t > 0:
            finish(0, t - 1)
        if t == tiles // 2:
            hand_on(BATCHES[1][2:])
    scale_inputs(1)
    finish(0, tiles - 1)
    hidden_units(1)
    for t in range(tiles):
        down_tile(1, t)
        if t > 0:
            finish(1, t - 1)
    finish(1, tiles - 1)

    for t in range(tiles):
        cols = slice(t * out_tile, (t + 1) * out_tile)
        for k in range(1, EXPERTS):
            back(t, k).wait_recv()
        o_ref[:, cols] = jnp.dot(placing[...], home[t], preferred_element_type=F32).astype(BF16)

    for k in range(1, EXPERTS):
        direct(k).wait_send()
    for k in range(EXPERTS):
        for j in range(1, split):
            handed(k, j).wait_send()
    for t in range(tiles):
        for b in range(len(BATCHES)):
            for j in range(1, split):
                share(b, t, j).wait_send()
        for k in range(1, EXPERTS):
            back(t, k).wait_send()


def per_device(
    tokens,
    expert_ids,
    member_ids,
    combine_weights,
    gate_weight,
    up_weight,
    down_weight,
    input_factors,
    hidden_factors,
    output_factors,
):
    n = lax.axis_size("expert")
    split = n // EXPERTS
    toks, width = tokens.shape
    units = gate_weight.shape[1]
    members = input_factors.shape[1]
    seg = EXPERTS * CAP
    all_rows = n * CAP
    batches = len(BATCHES)
    batch_rows = all_rows // batches
    out_tile = tile_of(width)
    tiles = width // out_tile
    vmem = pl.BlockSpec(memory_space=pltpu.VMEM)
    hbm = pl.BlockSpec(memory_space=pl.ANY)
    dma = pltpu.SemaphoreType.DMA
    return pl.pallas_call(
        functools.partial(kernel, n),
        out_shape=jax.ShapeDtypeStruct((toks, width), BF16),
        in_specs=[vmem] * 3 + [hbm] * 7,
        out_specs=vmem,
        scratch_shapes=[
            pltpu.VMEM((toks, width), BF16),
            pltpu.VMEM(hidden_factors.shape, F32),
            pltpu.VMEM((width, units), BF16),
            pltpu.VMEM((width, units), BF16),
            pltpu.VMEM((units, width), BF16),
            pltpu.VMEM((members, 2 * width), F32),
            pltpu.VMEM((members, width), F32),
            pltpu.VMEM((LANES, 2 * width), BF16),
            pltpu.VMEM((LANES, 2 * units), BF16),
            pltpu.VMEM((LANES, width), BF16),
            pltpu.VMEM((seg, width + LANES), BF16),
            pltpu.VMEM((all_rows, width + LANES), BF16),
            pltpu.VMEM((batch_rows, width), BF16),
            pltpu.VMEM((batch_rows, width), BF16),
            pltpu.VMEM((batch_rows, units), BF16),
            pltpu.VMEM((batches, tiles, batch_rows, out_tile), BF16),
            pltpu.VMEM((batches, tiles, split, seg // batches, out_tile), BF16),
            pltpu.VMEM((batches, tiles, seg // batches, out_tile), BF16),
            pltpu.VMEM((tiles, seg, out_tile), BF16),
            pltpu.VMEM((toks, seg), BF16),
            dma((3, CHUNKS)),
            dma((4,)),
            dma((EXPERTS,)),
            dma((EXPERTS,)),
            dma((batches, tiles, split)),
            dma((batches, tiles, split)),
            dma((tiles, EXPERTS)),
            dma((tiles, EXPERTS)),
            dma((EXPERTS, split)),
            dma((EXPERTS, split)),
        ],
        compiler_params=pltpu.CompilerParams(
            collective_id=0, has_side_effects=True, vmem_limit_bytes=67043328
        ),
        name="moe_step",
    )(
        expert_ids.T,
        member_ids.reshape(1, toks),
        combine_weights.T,
        tokens,
        hidden_factors,
        gate_weight,
        up_weight,
        down_weight,
        input_factors,
        output_factors,
    )


def solution(mesh):
    in_specs = (
        P(("groups", "expert"), None),
        P(("groups", "expert"), None),
        P(("groups", "expert")),
        P(("groups", "expert"), None),
        P(None, "expert"),
        P(None, "expert"),
        P("expert", None),
        P(),
        P(None, None, "expert"),
        P(),
    )
    out_specs = P(("groups", "expert"), None)
    return jax.shard_map(
        per_device, mesh=mesh, in_specs=in_specs, out_specs=out_specs, check_vma=False
    )
```

time: 52.6 us -> 48.7 us (0.926)
  local copies, waits for them, and re-layouts: 4.29 us -> 1.57 us
  Pallas kernels: 48.1 us -> 47 us
    unnamed x3 -> x1, local copies, waits for them, and re-layouts: 4.29 us -> 1.57 us
    pallas_call x1, Pallas kernels: 48.1 us -> 47 us  [per_device(): pl.pallas_call(functools.partial(kernel, n), out_shape=jax.ShapeDtypeStru...]
where the time goes in v2:
time: 48.7 us; the launch traced here: 48.6 us
  Pallas kernels  47 us (97%)
  local copies, waits for them, and re-layouts  1.57 us (3%)
    pallas_call x1, Pallas kernels, per_device(): pl.pallas_call(functools.partial(kernel, n), out_shape=jax.ShapeDtypeStru...  47 us
    unnamed x1, local copies, waits for them, and re-layouts  1.57 us

profile of v2, /device:TPU:0, one launch (start us, length us, event | category | flops | bytes accessed | tf_op | source)
XLA Modules:
  0.0 48.6 jit_solution(12102055908896190179)
XLA Ops:
  0.0 47.0 %moe_step.1 = bf16[32,2048]{1,0:T(8,128)(2,1)} custom-call(s32[2,32]{1,0:T(2,128)} %bitcast.3, s32[1,32]{1,0:T(1,128)} %bitcast.5, f32[2,32]{1,0:T(2,128)} %bitcast.4, bf16[32,2048]{1,0:T(8,128)(2,1)} %tok_hbm.1, f32[8,2,3584]{2,1,0:T(2,128)} %hidf_hbm.1, bf16[2048,3584]{1,0:T(8,128)(2,1)} %wg_hbm.1, bf16[2048,3584]{1,0:T(8,128)(2,1)} %wu_hbm.1, ...), custom_call_target="tpu_custom_call" | custom-call | tf_op jit(solution)/shard_map/moe_step/pallas_call | solution.py:401
  47.0 1.6 %copy.12 = bf16[32,2048]{1,0:T(8,128)(2,1)} copy(bf16[32,2048]{1,0:T(8,128)(2,1)} %moe_step.1) | data formatting | bytes 262144
